TPU v7x, 64 devices: a 2x2x8 block of a 4x4x8 slice. The times are simulated.
64 devices in a mesh: dp: 4 (over x, y), tp: 16 (over z, core).
Axes of the slice: x: 2, y: 2, z: 8, core: 2. Of those that a mesh axis runs over, the one named last changes fastest.
The devices are a block of a 4x4x8 slice.
Arguments:
- hidden: bfloat16 [24, 384, 6144], P('dp', 'tp'), parts along dimension 0
- lengths: int32 [24], P('dp'), parts along dimension 0
- rope_cos: float32 [24, 384, 32], P('dp'), parts along dimension 0
- rope_sin: float32 [24, 384, 32], P('dp'), parts along dimension 0
- cache_lat: bfloat16 [24, 2432, 512], P('dp'), parts along dimension 0
- cache_pe: bfloat16 [24, 2432, 64], P('dp'), parts along dimension 0
- norm_in: float32 [6144], replicated
- w_dq: bfloat16 [6144, 1536], replicated
- norm_q: float32 [1536], replicated
- w_dkv: bfloat16 [6144, 576], replicated
- norm_kv: float32 [512], replicated
- w_uq: bfloat16 [1536, 64, 192], P(None, 'tp')
- w_uk: bfloat16 [512, 64, 128], P(None, 'tp')
- w_uv: bfloat16 [512, 64, 128], P(None, 'tp')
- w_out: bfloat16 [8192, 6144], P('tp')
Outputs:
- output 1: bfloat16 [24, 384, 6144], P('dp', 'tp'), parts along dimension 0
- output 2: bfloat16 [24, 2432, 512], P('dp'), parts along dimension 0
- output 3: bfloat16 [24, 2432, 64], P('dp'), parts along dimension 0
There are 4 independent parts. A program takes and returns all parts, laid end to end along the dimension named above; an argument that names none is the same for every part.
All inputs are finite; a program needn't handle non-finite values.
Results may differ from a plain program's by a relative error of at most 0.0158764.
Values are sent between devices in bfloat16 or wider.
A program may use at most 768 MiB of HBM per device.

v0:
```python
import jax
import jax.numpy as jnp
from jax import lax
from jax.sharding import PartitionSpec as P


def rms_norm(values, gain_vec):
    inv_rms = lax.rsqrt(jnp.mean(values * values, axis=-1, keepdims=True) + 1e-6)
    return values * inv_rms * gain_vec


def apply_rope(values, cos_tab, sin_tab):
    half_dim = values.shape[-1] // 2
    lower_half = values[..., :half_dim]
    upper_half = values[..., half_dim:]
    return jnp.concatenate([lower_half * cos_tab - upper_half * sin_tab, upper_half * cos_tab + lower_half * sin_tab], axis=-1)


def write_rows(old_rows, new_rows, start_row):
    return lax.dynamic_update_slice(old_rows, new_rows, (start_row, 0))


def solution(mesh):
    def local_step(hidden, lengths, rope_cos, rope_sin, cache_lat, cache_pe, norm_in, w_dq, norm_q, w_dkv, norm_kv, w_uq, w_uk, w_uv, w_out):
        gathered = lax.all_gather(hidden, "tp", axis=1, tiled=True)
        chunk_len = gathered.shape[1]
        model_dim = gathered.shape[2]
        kv_rank, heads_local, nope_dim = w_uk.shape
        value_dim = w_uv.shape[2]
        rope_dim = cache_pe.shape[2]
        cache_len = cache_lat.shape[1]
        normed = rms_norm(gathered.astype(jnp.float32), norm_in).astype(jnp.bfloat16)
        q_latent = rms_norm(jnp.einsum("btd,dq->btq", normed, w_dq, preferred_element_type=jnp.float32), norm_q).astype(jnp.bfloat16)
        kv_proj = jnp.einsum("btd,dk->btk", normed, w_dkv, preferred_element_type=jnp.float32)
        new_lat = rms_norm(kv_proj[..., :kv_rank], norm_kv).astype(jnp.bfloat16)
        new_pe = apply_rope(kv_proj[..., kv_rank:], rope_cos, rope_sin).astype(jnp.bfloat16)
        lat_all = jax.vmap(write_rows)(cache_lat, new_lat, lengths)
        pe_all = jax.vmap(write_rows)(cache_pe, new_pe, lengths)
        q_full = jnp.einsum("btq,qhd->bthd", q_latent, w_uq, preferred_element_type=jnp.float32)
        q_nope = q_full[..., :nope_dim].astype(jnp.bfloat16)
        q_pe = apply_rope(q_full[..., nope_dim:], rope_cos[:, :, None, :], rope_sin[:, :, None, :]).astype(jnp.bfloat16)
        keys_nope = jnp.einsum("bsc,chd->bshd", lat_all, w_uk, preferred_element_type=jnp.float32).astype(jnp.bfloat16)
        values_all = jnp.einsum("bsc,chv->bshv", lat_all, w_uv, preferred_element_type=jnp.float32).astype(jnp.bfloat16)
        scores = jnp.einsum("bthd,bshd->bhts", q_nope, keys_nope, preferred_element_type=jnp.float32)
        scores = scores + jnp.einsum("bthr,bsr->bhts", q_pe, pe_all, preferred_element_type=jnp.float32)
        key_pos = jnp.arange(cache_len)[None, None, :]
        row_limit = lengths[:, None, None] + jnp.arange(chunk_len)[None, :, None] + 1
        visible = (key_pos < row_limit)[:, None, :, :]
        scores = jnp.where(visible, scores * ((nope_dim + rope_dim) ** -0.5), -1e30)
        attn_probs = jax.nn.softmax(scores, axis=-1).astype(jnp.bfloat16)
        attn_out = jnp.einsum("bhts,bshv->bthv", attn_probs, values_all, preferred_element_type=jnp.float32).astype(jnp.bfloat16)
        out_heads = w_out.reshape(heads_local, value_dim, model_dim)
        head_sum = jnp.einsum("bthv,hvd->btd", attn_out, out_heads, preferred_element_type=jnp.float32)
        reduced = lax.psum_scatter(head_sum, "tp", scatter_dimension=1, tiled=True)
        return (reduced + hidden.astype(jnp.float32)).astype(jnp.bfloat16), lat_all, pe_all

    spec_tok = P("dp", "tp", None)
    spec_len = P("dp")
    spec_seq = P("dp", None, None)
    spec_vec = P(None)
    spec_mat = P(None, None)
    spec_head = P(None, "tp", None)
    spec_rows = P("tp", None)
    in_specs = (spec_tok, spec_len, spec_seq, spec_seq, spec_seq, spec_seq, spec_vec, spec_mat, spec_vec, spec_mat, spec_vec, spec_head, spec_head, spec_head, spec_rows)
    return jax.shard_map(local_step, mesh=mesh, in_specs=in_specs, out_specs=(spec_tok, spec_seq, spec_seq), check_vma=False)
```

profile of v0, /device:TPU:21, one launch (start us, length us, event | category | flops | bytes accessed | tf_op | source)
XLA Modules:
  0.0 941.6 jit_solution(576204609625838301)
XLA Ops:
  7.3 3.0 copy.68
  10.3 13.6 %copy.67 = bf16[6,2432,512]{2,1,0:T(8,128)(2,1)} copy(bf16[6,2432,512]{2,1,0:T(8,128)(2,1)} %param.19) | data formatting | bytes 29884416
  24.2 5.7 iota_compare_fusion
  29.9 145.6 %all-gather.2.cloned.1.call-done = bf16[6,384,6144]{2,1,0:T(8,128)(2,1)} async-done(((bf16[6,24,6144]{2,1,0:T(8,128)(2,1)}), bf16[6,384,6144]{2,1,0:T(8,128)(2,1)}) %all-gather.2.cloned.1.call-update) | async-done | bytes 28311568 | tf_op jit(solution)/shard_map/all_gather | solution.py:25
  175.5 10.5 %fusion.3 = f32[6,384]{1,0:T(8,128)S(1)} fusion(bf16[6,384,6144]{2,1,0:T(8,128)(2,1)} %all-gather.2.cloned.1.call-done), kind=kLoop, calls=%fused_computation.15 | loop fusion | flops 42465024 | bytes 28320768 | tf_op jit(solution)/shard_map/reduce_sum | solution.py:8
  186.0 23.1 %fusion.9 = f32[6,384,576]{1,2,0:T(8,128)S(1)} fusion(bf16[6,384,6144]{2,1,0:T(8,128)(2,1)} %all-gather.2.cloned.1.call-done, f32[6144]{0:T(1024)S(1)} %copy-done.16, f32[6,384]{1,0:T(8,128)S(1)} %add_rsqrt_fusion.2, bf16[6144,576]{0,1:T(8,128)(2,1)} %param.24), kind=kOutput, calls=%fused_computation.21 | convolution fusion | flops 16364077056 | bytes 40731648 | tf_op jit(solution)/shard_map/btd,dk->btk/dot_general | solution.py:34
  211.7 54.6 %while.3 = (s32[]{:T(128)}, bf16[6,2432,64]{1,2,0:T(8,128)(2,1)}, s32[6,3]{0,1:T(4,128)S(1)}, bf16[6,384,64]{1,2,0:T(8,128)(2,1)S(1)}, s32[]{:T(128)}, /*index=5*/s32[3]{0:T(128)S(1)}, s32[]{:T(128)}) while((s32[]{:T(128)}, bf16[6,2432,64]{1,2,0:T(8,128)(2,1)}, s32[6,3]{0,1:T(4,128)S(1)}, bf16[6,384,64]{1,2,0:T(8,128)(2,1)S(1)}, s32[]{:T(128)}, ...), condition=%wide.while_cond.1, body=%wide.while_body.1.sunk | while | flops 24595 | bytes 245931 | solution.py:20
  226.7 3.0 dynamic-update-slice.7
  235.9 3.0 dynamic-update-slice.7
  266.3 54.9 %multiply_reduce_fusion = (f32[6,384]{1,0:T(8,128)S(1)}, f32[6,384,1536]{2,1,0:T(8,128)}) fusion(bf16[6144,1536]{1,0:T(8,128)(2,1)} %param.22, bf16[6,384,6144]{2,1,0:T(8,128)(2,1)} %all-gather.2.cloned.1.call-done, f32[6144]{0:T(1024)S(1)} %copy-done.16, f32[6,384]{1,0:T(8,128)S(1)} %add_rsqrt_fusion.2), kind=kOutput, calls=%fused_computation.31 | convolution fusion | flops 43550240768 | bytes 61384704 | tf_op jit(solution)/shard_map/btd,dq->btq/dot_general | solution.py:33
  321.3 9.3 fusion.26
  334.1 74.0 %while.2 = (s32[]{:T(128)}, bf16[6,2432,512]{2,1,0:T(8,128)(2,1)}, s32[6,3]{0,1:T(4,128)S(1)}, bf16[6,384,512]{1,2,0:T(8,128)(2,1)}, s32[]{:T(128)}, /*index=5*/s32[3]{0:T(128)S(1)}, s32[]{:T(128)}) while((s32[]{:T(128)}, bf16[6,2432,512]{2,1,0:T(8,128)(2,1)}, s32[6,3]{0,1:T(4,128)S(1)}, bf16[6,384,512]{1,2,0:T(8,128)(2,1)}, s32[]{:T(128)}, ...), condition=%wide.while_cond, body=%wide.while_body.sunk | while | flops 196627 | bytes 3539115 | solution.py:20
  338.7 3.1 dynamic-slice_select_fusion.4
  341.8 4.1 dynamic-update-slice.6
  350.6 3.1 dynamic-slice_select_fusion.4
  353.7 4.7 dynamic-update-slice.6
  363.0 3.1 dynamic-slice_select_fusion.4
  366.1 4.7 dynamic-update-slice.6
  375.4 3.1 dynamic-slice_select_fusion.4
  378.5 4.7 dynamic-update-slice.6
  387.9 3.1 dynamic-slice_select_fusion.4
  391.0 4.7 dynamic-update-slice.6
  400.3 3.1 dynamic-slice_select_fusion.4
  403.4 4.7 dynamic-update-slice.6
  408.1 16.5 %fusion.22 = bf16[6,2432,4,128]{3,1,2,0:T(8,128)(2,1)} fusion(bf16[6,2432,512]{2,1,0:T(8,128)(2,1)} %get-tuple-element.8, bf16[512,4,128,1]{2,1,0,3:T(4,128)(2,1)S(1)} %bitcast.96), kind=kOutput, calls=%fused_computation.32 | convolution fusion | flops 7657881600 | bytes 30408704 | tf_op jit(solution)/shard_map/bsc,chv->bshv/dot_general | solution.py:43
  424.6 32.5 %copy.32 = bf16[6,2432,4,128]{3,2,1,0:T(4,128)(2,1)} copy(bf16[6,2432,4,128]{3,1,2,0:T(8,128)(2,1)} %fusion.22) | data formatting | bytes 29884416
  457.1 32.2 %fusion.38 = f32[6,2432,384,4]{1,2,3,0:T(8,128)} fusion(bf16[6,2432,64]{1,2,0:T(8,128)(2,1)S(1)} %copy-done.4, bf16[6,384,4,32]{1,3,2,0:T(8,128)(2,1)S(1)} %get-tuple-element.46, bf16[6,384,4,32]{1,3,2,0:T(8,128)(2,1)S(1)} %get-tuple-element.45), kind=kOutput, calls=%fused_computation.45 | convolution fusion | flops 2871263232 | bytes 92700672 | tf_op jit(solution)/shard_map/bthr,bsr->bhts/dot_general | solution.py:45
  489.3 85.7 %fusion.50 = (f32[6,4,384]{2,1,0:T(4,128)S(1)}, f32[6,4,384,2432]{3,2,1,0:T(8,128)}) fusion(f32[6,2432,384,4]{1,2,3,0:T(8,128)} %fusion.38, pred[6,384,2432]{2,1,0:T(8,128)(4,1)} %iota_compare_fusion, bf16[6,2432,512]{2,1,0:T(8,128)(2,1)} %get-tuple-element.8, f32[6,384,4,192]{1,3,2,0:T(8,128)} %copy-done.9, bf16[512,4,128,1]{2,1,0,3:T(4,128)(2,1)} %bitcast.97), kind=kOutput, calls=%fused_computation.68 | convolution fusion | flops 13507758080 | bytes 202772480 | tf_op jit(solution)/shard_map/sub | solution.py:50
  575.0 36.3 %fusion.64 = bf16[6,384,4,128]{3,1,2,0:T(8,128)(2,1)S(1)} fusion(bf16[6,2432,4,128]{3,2,1,0:T(4,128)(2,1)} %copy.32, f32[6,4,384,2432]{3,2,1,0:T(8,128)} %get-tuple-element.52, f32[6,4,384]{2,1,0:T(4,128)S(1)} %get-tuple-element.51), kind=kOutput, calls=%fused_computation.42.clone.1 | convolution fusion | flops 5783814144 | bytes 106991616 | tf_op jit(solution)/shard_map/bhts,bshv->bthv/dot_general | solution.py:51
  611.3 23.5 %convolution_bitcast_fusion = f32[6,384,6144]{2,1,0:T(8,128)} fusion(bf16[4,128,6144,1]{2,1,0,3:T(8,128)(2,1)} %bitcast.95, bf16[6,384,4,128]{3,1,2,0:T(8,128)(2,1)S(1)} %fusion.64), kind=kOutput, calls=%fused_computation.22 | convolution fusion | flops 14495514624 | bytes 65273856 | tf_op jit(solution)/shard_map/bthv,hvd->btd/dot_general | solution.py:53
  634.9 295.5 %reduce-scatter.2.cloned.1.call-done = f32[6,24,6144]{2,1,0:T(8,128)} async-done(((f32[6,384,6144]{2,1,0:T(8,128)}), f32[6,24,6144]{2,1,0:T(8,128)}) %reduce-scatter.2.cloned.1.call-update) | async-done | bytes 3538960 | tf_op jit(solution)/shard_map/reduce_scatter | solution.py:54
  930.4 4.1 add_convert_fusion
  (111 shorter events, 82.7 us)
Async XLA Ops:
  7.2 314.0 %copy-start = (bf16[1536,4,192]{0,2,1:T(8,128)(2,1)S(1)}, bf16[1536,4,192]{0,2,1:T(8,128)(2,1)}, u32[]{:S(2)}) copy-start(bf16[1536,4,192]{0,2,1:T(8,128)(2,1)} %param.26) | copy-start | bytes 7077892
  7.2 168.3 %all-gather.2.cloned.1.call-start = ((), (), s32[]{:S(2)}) async-start(), calls=%async_computation.1 | async-start | bytes 30081024 | tf_op jit(solution)/shard_map/all_gather | solution.py:25
  10.3 13.7 %copy-start.13 = (s32[6]{0:T(128)S(1)}, s32[6]{0:T(128)}, u32[]{:S(2)}) copy-start(s32[6]{0:T(128)} %param.16) | copy-start | bytes 76
  10.3 13.7 %copy-start.14 = (s32[2]{0:T(128)S(1)}, s32[2]{0:T(128)}, u32[]{:S(2)}) copy-start(s32[2]{0:T(128)} %constant.14.clone.1) | copy-start | bytes 28
  23.9 906.4 %reduce-scatter.2.cloned.1.call-start = ((), (), s32[]{:S(2)}) async-start(), calls=%async_computation.2 | async-start | bytes 60162048 | tf_op jit(solution)/shard_map/reduce_scatter | solution.py:54
  29.9 156.1 %copy-start.16 = (f32[6144]{0:T(1024)S(1)}, f32[6144]{0:T(1024)}, u32[]{:S(2)}) copy-start(f32[6144]{0:T(1024)} %param.21) | copy-start | bytes 73732
  186.0 25.6 %copy-start.5 = (f32[6,384,32]{1,2,0:T(8,128)S(1)}, f32[6,384,32]{1,2,0:T(8,128)}, u32[]{:S(2)}) copy-start(f32[6,384,32]{1,2,0:T(8,128)} %param.18) | copy-start | bytes 884740
  186.0 25.6 %copy-start.7 = (f32[6,384,32]{1,2,0:T(8,128)S(1)}, f32[6,384,32]{1,2,0:T(8,128)}, u32[]{:S(2)}) copy-start(f32[6,384,32]{1,2,0:T(8,128)} %param.17) | copy-start | bytes 884740
  186.0 25.7 %copy-start.10 = (s32[3]{0:T(128)S(1)}, s32[3]{0:T(128)}, u32[]{:S(2)}) copy-start(s32[3]{0:T(128)} %constant.114) | copy-start | bytes 40
  209.1 2.4 copy-start.2
  266.3 54.9 %copy-start.17 = (f32[1536]{0:T(1024)S(1)}, f32[1536]{0:T(1024)}, u32[]{:S(2)}) copy-start(f32[1536]{0:T(1024)} %param.23) | copy-start | bytes 18436
  321.2 9.3 copy-start.6
  321.3 9.3 copy-start.8
  321.3 9.7 %copy-start.11 = (f32[6,384]{1,0:T(8,128)S(1)}, f32[6,384]{1,0:T(8,128)}, u32[]{:S(2)}) copy-start(f32[6,384]{1,0:T(8,128)} %multiply_reduce_fusion.1) | copy-start | bytes 27652
  321.3 9.8 %copy-start.3 = (f32[6,384,576]{1,2,0:T(8,128)S(1)}, f32[6,384,576]{1,2,0:T(8,128)}, u32[]{:S(2)}) copy-start(f32[6,384,576]{1,2,0:T(8,128)} %copy-done.2) | copy-start | bytes 15925252
  321.3 9.8 %copy-start.12 = (f32[512]{0:T(512)S(1)}, f32[512]{0:T(512)}, u32[]{:S(2)}) copy-start(f32[512]{0:T(512)} %param.25) | copy-start | bytes 6148
  330.6 3.5 copy-start.9
  330.6 77.5 %copy-start.15 = (bf16[512,4,128]{2,1,0:T(4,128)(2,1)S(1)}, bf16[512,4,128]{2,1,0:T(4,128)(2,1)}, u32[]{:S(2)}) copy-start(bf16[512,4,128]{2,1,0:T(4,128)(2,1)} %param.28) | copy-start | bytes 1572868
  424.6 32.5 %copy-start.4 = (bf16[6,2432,64]{1,2,0:T(8,128)(2,1)S(1)}, bf16[6,2432,64]{1,2,0:T(8,128)(2,1)}, u32[]{:S(2)}) copy-start(bf16[6,2432,64]{1,2,0:T(8,128)(2,1)} %get-tuple-element.16) | copy-start | bytes 5603332
  634.9 299.6 %copy-start.1 = (bf16[1536,4,192]{0,2,1:T(8,128)(2,1)S(1)}, bf16[1536,4,192]{0,2,1:T(8,128)(2,1)}, u32[]{:S(2)}) copy-start(bf16[1536,4,192]{0,2,1:T(8,128)(2,1)} %param.26) | copy-start | bytes 7077892
Sparse Core Ops, SparseCore 0:
  24.1 151.3 all-gather.1
  635.0 295.3 reduce-scatter.1
where the time goes:
time: 948 us; the launch traced here: 942 us
  waiting for transfers between devices  441 us (47%)
  matrix products  281 us (30%)
  local copies, waits for them, and re-layouts  112 us (12%)
  other arithmetic  92.5 us (10%)
  between operations  14.6 us (2%)
    reduce_scatter x1, waiting for transfers between devices, local_step(): reduced = lax.psum_scatter(head_sum, 'tp', scatter_dimension=1, tiled=True)  295 us
    all_gather x1, waiting for transfers between devices, local_step(): gathered = lax.all_gather(hidden, 'tp', axis=1, tiled=True)  146 us
    sub x1, matrix products, local_step(): attn_probs = jax.nn.softmax(scores, axis=-1).astype(jnp.bfloat16)  85.7 us
    scatter x24, other arithmetic  67.9 us
    scatter x48, local copies, waits for them, and re-layouts  60.6 us
    dot_general x1, matrix products, local_step(): jnp.einsum('btd,dq->btq', normed, w_dq, preferred_element_type=jnp.float32)  54.9 us
    unnamed x40, local copies, waits for them, and re-layouts  51 us
    dot_general x1, matrix products, local_step(): jnp.einsum('bhts,bshv->bthv', attn_probs, values_all, preferred_element_t...  36.3 us
  transfers between devices with their start and end apart: 2, of which 2 were waited for; matrix products, arithmetic and copies ran while one was open for 1% of the time, Pallas kernels for 0%

commit v1 on v0

v1 whole, which is shorter than its diff:
```python
import jax
import jax.numpy as jnp
from jax import lax
from jax.sharding import PartitionSpec as P


def rms_norm(values, gain_vec):
    inv_rms = lax.rsqrt(jnp.mean(values * values, axis=-1, keepdims=True) + 1e-6)
    return values * inv_rms * gain_vec


def apply_rope(values, cos_tab, sin_tab):
    half_dim = values.shape[-1] // 2
    lower_half = values[..., :half_dim]
    upper_half = values[..., half_dim:]
    return jnp.concatenate([lower_half * cos_tab - upper_half * sin_tab, upper_half * cos_tab + lower_half * sin_tab], axis=-1)


def dot(a, b):
    return jnp.dot(a, b, preferred_element_type=jnp.float32)


def solution(mesh):
    tp_size = mesh.shape["tp"]

    def local_step(hidden, lengths, rope_cos, rope_sin, cache_lat, cache_pe, norm_in, w_dq, norm_q, w_dkv, norm_kv, w_uq, w_uk, w_uv, w_out):
        seqs, own_len, model_dim = hidden.shape
        chunk_len = own_len * tp_size
        kv_rank, heads_local, nope_dim = w_uk.shape
        value_dim = w_uv.shape[2]
        rope_dim = cache_pe.shape[2]
        cache_len = cache_lat.shape[1]
        me = lax.axis_index("tp")
        own_cos = lax.dynamic_slice_in_dim(rope_cos, me * own_len, own_len, axis=1)
        own_sin = lax.dynamic_slice_in_dim(rope_sin, me * own_len, own_len, axis=1)

        normed = rms_norm(hidden.astype(jnp.float32), norm_in).astype(jnp.bfloat16).reshape(seqs * own_len, model_dim)
        kv_proj = dot(normed, w_dkv).reshape(seqs, own_len, kv_rank + rope_dim)
        own_lat = rms_norm(kv_proj[..., :kv_rank], norm_kv).astype(jnp.bfloat16)
        own_pe = apply_rope(kv_proj[..., kv_rank:], own_cos, own_sin).astype(jnp.bfloat16)
        own_q = rms_norm(dot(normed, w_dq), norm_q).astype(jnp.bfloat16).reshape(seqs, own_len, -1)
        new_kv = lax.all_gather(jnp.concatenate([own_lat, own_pe], axis=-1), "tp", axis=1, tiled=True)
        q_latent = lax.all_gather(own_q, "tp", axis=1, tiled=True)

        lat_all, pe_all = cache_lat, cache_pe
        for b in range(seqs):
            lat_all = lax.dynamic_update_slice(lat_all, new_kv[b : b + 1, :, :kv_rank], (b, lengths[b], 0))
            pe_all = lax.dynamic_update_slice(pe_all, new_kv[b : b + 1, :, kv_rank:], (b, lengths[b], 0))

        scale = (nope_dim + rope_dim) ** -0.5
        outs = []
        for b in range(seqs):
            q_full = jnp.einsum("tq,qhd->htd", q_latent[b], w_uq, preferred_element_type=jnp.float32)
            q_nope = q_full[..., :nope_dim].astype(jnp.bfloat16)
            q_pe = apply_rope(q_full[..., nope_dim:], rope_cos[b], rope_sin[b]).astype(jnp.bfloat16)
            keys_nope = jnp.einsum("sc,chd->hsd", lat_all[b], w_uk, preferred_element_type=jnp.float32).astype(jnp.bfloat16)
            values = jnp.einsum("sc,chv->hsv", lat_all[b], w_uv, preferred_element_type=jnp.float32).astype(jnp.bfloat16)
            keys = jnp.concatenate([keys_nope, jnp.broadcast_to(pe_all[b][None], (heads_local, cache_len, rope_dim))], axis=-1)
            queries = jnp.concatenate([q_nope, q_pe], axis=-1)
            scores = jnp.einsum("htd,hsd->hts", queries, keys, preferred_element_type=jnp.float32)
            visible = jnp.arange(cache_len)[None, :] < lengths[b] + jnp.arange(chunk_len)[:, None] + 1
            scores = jnp.where(visible[None], scores * scale, -1e30)
            probs = jax.nn.softmax(scores, axis=-1).astype(jnp.bfloat16)
            attn = jnp.einsum("hts,hsv->thv", probs, values, preferred_element_type=jnp.float32).astype(jnp.bfloat16)
            head_sum = dot(attn.reshape(chunk_len, heads_local * value_dim), w_out)
            reduced = lax.psum_scatter(head_sum, "tp", scatter_dimension=0, tiled=True)
            outs.append((reduced + hidden[b].astype(jnp.float32)).astype(jnp.bfloat16))
        return jnp.stack(outs), lat_all, pe_all

    spec_tok = P("dp", "tp", None)
    spec_len = P("dp")
    spec_seq = P("dp", None, None)
    spec_vec = P(None)
    spec_mat = P(None, None)
    spec_head = P(None, "tp", None)
    spec_rows = P("tp", None)
    in_specs = (spec_tok, spec_len, spec_seq, spec_seq, spec_seq, spec_seq, spec_vec, spec_mat, spec_vec, spec_mat, spec_vec, spec_head, spec_head, spec_head, spec_rows)
    return jax.shard_map(local_step, mesh=mesh, in_specs=in_specs, out_specs=(spec_tok, spec_seq, spec_seq), check_vma=False)
```

time: 948 us -> 616 us (0.65)
  waiting for transfers between devices: 441 us -> 149 us
  matrix products: 281 us -> 212 us
  other arithmetic: 92.5 us -> 154 us
  local copies, waits for them, and re-layouts: 112 us -> 64 us
  between operations: 14.6 us -> 26.3 us
    reduce_scatter x1 -> x6, waiting for transfers between devices: 295 us -> 130 us  [local_step(): reduced = lax.psum_scatter(head_sum, 'tp', scatter_dimension=0, tiled=True)]
    all_gather x1 -> x2, waiting for transfers between devices: 146 us -> 19.1 us  [the longest x1 16.4 us: local_step(): lax.all_gather(jnp.concatenate([own_lat, own_pe], axis=-1), 'tp', axis=1,...]
    sub x0 -> x6, other arithmetic: none -> 125 us  [local_step(): probs = jax.nn.softmax(scores, axis=-1).astype(jnp.bfloat16)]
    sub x1 -> x0, matrix products: 85.7 us -> none  [local_step(): attn_probs = jax.nn.softmax(scores, axis=-1).astype(jnp.bfloat16)]
    scatter x25 -> x0, other arithmetic: 67.9 us -> none
    scatter x48 -> x0, local copies, waits for them, and re-layouts: 60.6 us -> none
    unnamed x40 -> x68, local copies, waits for them, and re-layouts: 51 us -> 17.7 us
    dynamic_update_slice x0 -> x12, local copies, waits for them, and re-layouts: none -> 30.7 us  [the longest x6 20.5 us: local_step(): lax.dynamic_update_slice(lat_all, new_kv[b:b + 1, :, :kv_rank], (b, lengt...]
  transfers between devices with their start and end apart: 2 -> 8, of which waited for: 2 -> 4; matrix products, arithmetic and copies ran while one was open for 1% -> 57% of each run, Pallas kernels for 0% -> 0%
where the time goes in v1:
time: 616 us; the launch traced here: 607 us
  matrix products  212 us (34%)
  other arithmetic  154 us (25%)
  waiting for transfers between devices  149 us (24%)
  local copies, waits for them, and re-layouts  64 us (10%)
  between operations  26.3 us (4%)
    reduce_scatter x6, waiting for transfers between devices, local_step(): reduced = lax.psum_scatter(head_sum, 'tp', scatter_dimension=0, tiled=True)  130 us
    sub x6, other arithmetic, local_step(): probs = jax.nn.softmax(scores, axis=-1).astype(jnp.bfloat16)  125 us
    dot_general x8, matrix products, dot(): return jnp.dot(a, b, preferred_element_type=jnp.float32)  69.3 us
    dot_general x6, matrix products, local_step(): jnp.einsum('hts,hsv->thv', probs, values, preferred_element_type=jnp.floa...  59.9 us
    dot_general x6, matrix products, local_step(): jnp.einsum('htd,hsd->hts', queries, keys, preferred_element_type=jnp.floa...  45.2 us
    dot_general x6, matrix products, local_step(): jnp.einsum('sc,chd->hsd', lat_all[b], w_uk, preferred_element_type=jnp.fl...  21.6 us
    dynamic_update_slice x6, local copies, waits for them, and re-layouts, local_step(): lax.dynamic_update_slice(lat_all, new_kv[b:b + 1, :, :kv_rank], (b, lengt...  20.5 us
    unnamed x68, local copies, waits for them, and re-layouts  17.7 us
  transfers between devices with their start and end apart: 8, of which 4 were waited for; matrix products, arithmetic and copies ran while one was open for 57% of the time, Pallas kernels for 0%

profile of v1, /device:TPU:21, one launch (start us, length us, event | category | flops | bytes accessed | tf_op | source)
XLA Modules:
  0.0 606.7 jit_solution(8863784506043329814)
XLA Ops:
  7.3 13.8 %copy.79 = bf16[6,2432,512]{2,1,0:T(8,128)(2,1)} copy(bf16[6,2432,512]{2,1,0:T(8,128)(2,1)} %param.19) | data formatting | bytes 29884416
  26.7 6.2 %fusion.36 = f32[6,24,576]{2,1,0:T(8,128)S(1)} fusion(bf16[6,24,6144]{2,1,0:T(8,128)(2,1)S(1)} %fusion.76, bf16[6144,576]{0,1:T(8,128)(2,1)} %param.24), kind=kOutput, calls=%fused_computation.54 | convolution fusion | flops 1019215872 | bytes 9179136 | tf_op jit(solution)/shard_map/dot_general | solution.py:20
  34.2 8.7 %multiply_reduce_fusion = (f32[144]{0:T(256)S(1)}, f32[144,1536]{1,0:T(8,128)S(1)}) fusion(bf16[144,6144]{1,0:T(8,128)(2,1)} %bitcast.254, bf16[6144,1536]{1,0:T(8,128)(2,1)} %param.22), kind=kOutput, calls=%fused_computation.140 | convolution fusion | flops 2718351104 | bytes 21529152 | tf_op jit(solution)/shard_map/dot_general | solution.py:20
  59.5 16.4 %all-gather.3.cloned.1.call-done = bf16[6,384,576]{2,1,0:T(8,128)(2,1)} async-done(((bf16[6,24,576]{2,1,0:T(8,128)(2,1)}), bf16[6,384,576]{2,1,0:T(8,128)(2,1)}) %all-gather.3.cloned.1.call-update) | async-done | bytes 2654224 | tf_op jit(solution)/shard_map/all_gather | solution.py:42
  89.0 3.5 dynamic_update_slice.37
  114.8 5.0 fusion.39
  130.1 7.5 %fusion.50 = f32[4,384,2432]{2,1,0:T(8,128)} fusion(bf16[4,2432,64]{1,2,0:T(8,128)(2,1)S(1)} %broadcast_in_dim.122, bf16[4,2432,128]{1,2,0:T(8,128)(2,1)S(1)} %copy-done.3, bf16[4,384,32]{1,2,0:T(8,128)(2,1)S(1)} %get-tuple-element.73, bf16[4,384,32]{1,2,0:T(8,128)(2,1)S(1)} %get-tuple-element.74, bf16[4,384,128]{1,2,0:T(8,128)(2,1)S(1)} %slice.503), kind=kOutput, calls=%fused_computation.82 | convolution fusion | flops 1443692544 | bytes 19267584 | tf_op jit(solution)/shard_map/htd,hsd->hts/dot_general | solution.py:60
  137.6 21.2 %fusion.176 = (f32[4,384]{1,0:T(4,128)S(1)}, f32[4,384,2432]{2,1,0:T(8,128)}) fusion(f32[4,384,2432]{2,1,0:T(8,128)} %fusion.50, pred[384,2432]{1,0:T(8,128)(4,1)} %iota_compare_fusion.5), kind=kOutput, calls=%fused_computation.280 | output fusion | flops 22415744 | bytes 30824448 | tf_op jit(solution)/shard_map/sub | solution.py:63
  158.7 10.6 %fusion.82 = bf16[4,128,384]{2,1,0:T(8,128)(2,1)} fusion(f32[4,384,2432]{2,1,0:T(8,128)} %get-tuple-element.56, f32[4,384]{1,0:T(4,128)S(1)} %get-tuple-element.55, bf16[6,2432,512]{2,1,0:T(8,128)(2,1)} %dynamic_update_slice.41, bf16[512,4,128]{2,1,0:T(4,128)(2,1)} %param.28), kind=kOutput, calls=%fused_computation.126 | convolution fusion | flops 2240282624 | bytes 18356224 | tf_op jit(solution)/shard_map/hts,hsv->thv/dot_general | solution.py:64
  169.3 9.2 %fusion.182 = f32[384,6144]{1,0:T(8,128)} fusion(bf16[384,512]{0,1:T(8,128)(2,1)} %bitcast.268, bf16[512,6144]{1,0:T(8,128)(2,1)} %param.29), kind=kOutput, calls=%fused_computation.286 | convolution fusion | flops 2415919104 | bytes 16121856 | tf_op jit(solution)/shard_map/dot_general | solution.py:20
  185.5 7.5 %fusion.54 = f32[4,384,2432]{2,1,0:T(8,128)} fusion(bf16[4,2432,64]{1,2,0:T(8,128)(2,1)S(1)} %broadcast_in_dim.126, bf16[4,2432,128]{1,2,0:T(8,128)(2,1)S(1)} %fusion.41, bf16[4,384,32]{1,2,0:T(8,128)(2,1)S(1)} %get-tuple-element.30, bf16[4,384,32]{1,2,0:T(8,128)(2,1)S(1)} %get-tuple-element.29, bf16[4,384,128]{1,2,0:T(8,128)(2,1)S(1)} %slice.502), kind=kOutput, calls=%fused_computation.86 | convolution fusion | flops 1443692544 | bytes 19267584 | tf_op jit(solution)/shard_map/htd,hsd->hts/dot_general | solution.py:60
  193.0 21.1 %fusion.177 = (f32[4,384]{1,0:T(4,128)S(1)}, f32[4,384,2432]{2,1,0:T(8,128)}) fusion(f32[4,384,2432]{2,1,0:T(8,128)} %fusion.54, pred[384,2432]{1,0:T(8,128)(4,1)} %iota_compare_fusion.4), kind=kOutput, calls=%fused_computation.281 | output fusion | flops 22415744 | bytes 30824448 | tf_op jit(solution)/shard_map/sub | solution.py:63
  214.1 9.9 %fusion.81 = bf16[4,128,384]{2,1,0:T(8,128)(2,1)S(1)} fusion(f32[4,384,2432]{2,1,0:T(8,128)} %get-tuple-element.58, f32[4,384]{1,0:T(4,128)S(1)} %get-tuple-element.57, bf16[6,2432,512]{2,1,0:T(8,128)(2,1)} %dynamic_update_slice.41, bf16[512,4,128]{2,1,0:T(4,128)(2,1)} %param.28), kind=kOutput, calls=%fused_computation.125 | convolution fusion | flops 2240282624 | bytes 18356224 | tf_op jit(solution)/shard_map/hts,hsv->thv/dot_general | solution.py:64
  224.0 9.1 %fusion.183 = f32[384,6144]{1,0:T(8,128)} fusion(bf16[384,512]{0,1:T(8,128)(2,1)S(1)} %bitcast.269, bf16[512,6144]{1,0:T(8,128)(2,1)} %param.29), kind=kOutput, calls=%fused_computation.287 | convolution fusion | flops 2415919104 | bytes 16121856 | tf_op jit(solution)/shard_map/dot_general | solution.py:20
  245.3 7.5 %fusion.58 = f32[4,384,2432]{2,1,0:T(8,128)} fusion(bf16[4,2432,64]{1,2,0:T(8,128)(2,1)S(1)} %broadcast_in_dim.129, bf16[4,2432,128]{1,2,0:T(8,128)(2,1)S(1)} %fusion.43, bf16[4,384,32]{1,2,0:T(8,128)(2,1)S(1)} %get-tuple-element.71, bf16[4,384,32]{1,2,0:T(8,128)(2,1)S(1)} %get-tuple-element.72, bf16[4,384,128]{1,2,0:T(8,128)(2,1)S(1)} %slice.501), kind=kOutput, calls=%fused_computation.90 | convolution fusion | flops 1443692544 | bytes 19267584 | tf_op jit(solution)/shard_map/htd,hsd->hts/dot_general | solution.py:60
  252.9 21.4 %fusion.178 = (f32[4,384]{1,0:T(4,128)S(1)}, f32[4,384,2432]{2,1,0:T(8,128)}) fusion(f32[4,384,2432]{2,1,0:T(8,128)} %fusion.58, pred[384,2432]{1,0:T(8,128)(4,1)} %iota_compare_fusion.3), kind=kOutput, calls=%fused_computation.282 | output fusion | flops 22415744 | bytes 30824448 | tf_op jit(solution)/shard_map/sub | solution.py:63
  274.3 9.9 %fusion.80 = bf16[4,128,384]{2,1,0:T(8,128)(2,1)S(1)} fusion(f32[4,384,2432]{2,1,0:T(8,128)} %get-tuple-element.60, f32[4,384]{1,0:T(4,128)S(1)} %get-tuple-element.59, bf16[6,2432,512]{2,1,0:T(8,128)(2,1)} %dynamic_update_slice.41, bf16[512,4,128]{2,1,0:T(4,128)(2,1)} %param.28), kind=kOutput, calls=%fused_computation.124 | convolution fusion | flops 2240282624 | bytes 18356224 | tf_op jit(solution)/shard_map/hts,hsv->thv/dot_general | solution.py:64
  284.1 8.9 %fusion.184 = f32[384,6144]{1,0:T(8,128)} fusion(bf16[384,512]{0,1:T(8,128)(2,1)S(1)} %bitcast.270, bf16[512,6144]{1,0:T(8,128)(2,1)} %param.29), kind=kOutput, calls=%fused_computation.288 | convolution fusion | flops 2415919104 | bytes 16121856 | tf_op jit(solution)/shard_map/dot_general | solution.py:20
  300.1 7.5 %fusion.62 = f32[4,384,2432]{2,1,0:T(8,128)} fusion(bf16[4,2432,64]{1,2,0:T(8,128)(2,1)S(1)} %broadcast_in_dim.132, bf16[4,2432,128]{1,2,0:T(8,128)(2,1)S(1)} %fusion.45, bf16[4,384,32]{1,2,0:T(8,128)(2,1)S(1)} %get-tuple-element.26, bf16[4,384,32]{1,2,0:T(8,128)(2,1)S(1)} %get-tuple-element.25, bf16[4,384,128]{1,2,0:T(8,128)(2,1)S(1)} %slice.500), kind=kOutput, calls=%fused_computation.94 | convolution fusion | flops 1443692544 | bytes 19267584 | tf_op jit(solution)/shard_map/htd,hsd->hts/dot_general | solution.py:60
  307.6 20.3 %fusion.179 = (f32[4,384]{1,0:T(4,128)S(1)}, f32[4,384,2432]{2,1,0:T(8,128)}) fusion(f32[4,384,2432]{2,1,0:T(8,128)} %fusion.62, pred[384,2432]{1,0:T(8,128)(4,1)S(1)} %copy-done.8), kind=kOutput, calls=%fused_computation.283 | output fusion | flops 22415744 | bytes 30824448 | tf_op jit(solution)/shard_map/sub | solution.py:63
  328.0 9.9 %fusion.79 = bf16[4,128,384]{2,1,0:T(8,128)(2,1)S(1)} fusion(f32[4,384,2432]{2,1,0:T(8,128)} %get-tuple-element.62, f32[4,384]{1,0:T(4,128)S(1)} %get-tuple-element.61, bf16[6,2432,512]{2,1,0:T(8,128)(2,1)} %dynamic_update_slice.41, bf16[512,4,128]{2,1,0:T(4,128)(2,1)} %param.28), kind=kOutput, calls=%fused_computation.123 | convolution fusion | flops 2240282624 | bytes 18356224 | tf_op jit(solution)/shard_map/hts,hsv->thv/dot_general | solution.py:64
  337.8 9.0 %fusion.185 = f32[384,6144]{1,0:T(8,128)} fusion(bf16[384,512]{0,1:T(8,128)(2,1)S(1)} %bitcast.271, bf16[512,6144]{1,0:T(8,128)(2,1)} %param.29), kind=kOutput, calls=%fused_computation.289 | convolution fusion | flops 2415919104 | bytes 16121856 | tf_op jit(solution)/shard_map/dot_general | solution.py:20
  358.3 7.5 %fusion.66 = f32[4,384,2432]{2,1,0:T(8,128)} fusion(bf16[4,2432,64]{1,2,0:T(8,128)(2,1)S(1)} %broadcast_in_dim.135, bf16[4,2432,128]{1,2,0:T(8,128)(2,1)S(1)} %fusion.47, bf16[4,384,32]{1,2,0:T(8,128)(2,1)S(1)} %get-tuple-element.69, bf16[4,384,32]{1,2,0:T(8,128)(2,1)S(1)} %get-tuple-element.70, bf16[4,384,128]{1,2,0:T(8,128)(2,1)S(1)} %slice.499), kind=kOutput, calls=%fused_computation.98 | convolution fusion | flops 1443692544 | bytes 19267584 | tf_op jit(solution)/shard_map/htd,hsd->hts/dot_general | solution.py:60
  365.9 20.7 %fusion.180 = (f32[4,384]{1,0:T(4,128)S(1)}, f32[4,384,2432]{2,1,0:T(8,128)}) fusion(f32[4,384,2432]{2,1,0:T(8,128)} %fusion.66, pred[384,2432]{1,0:T(8,128)(4,1)S(1)} %iota_compare_fusion.1), kind=kOutput, calls=%fused_computation.284 | output fusion | flops 22415744 | bytes 30824448 | tf_op jit(solution)/shard_map/sub | solution.py:63
  386.6 9.9 %fusion.78 = bf16[4,128,384]{2,1,0:T(8,128)(2,1)S(1)} fusion(f32[4,384,2432]{2,1,0:T(8,128)} %get-tuple-element.64, f32[4,384]{1,0:T(4,128)S(1)} %get-tuple-element.63, bf16[6,2432,512]{2,1,0:T(8,128)(2,1)} %dynamic_update_slice.41, bf16[512,4,128]{2,1,0:T(4,128)(2,1)} %param.28), kind=kOutput, calls=%fused_computation.122 | convolution fusion | flops 2240282624 | bytes 18356224 | tf_op jit(solution)/shard_map/hts,hsv->thv/dot_general | solution.py:64
  396.4 9.1 %fusion.186 = f32[384,6144]{1,0:T(8,128)} fusion(bf16[384,512]{0,1:T(8,128)(2,1)S(1)} %bitcast.272, bf16[512,6144]{1,0:T(8,128)(2,1)} %param.29), kind=kOutput, calls=%fused_computation.290 | convolution fusion | flops 2415919104 | bytes 16121856 | tf_op jit(solution)/shard_map/dot_general | solution.py:20
  411.8 7.5 %fusion.70 = f32[4,384,2432]{2,1,0:T(8,128)} fusion(bf16[4,2432,64]{1,2,0:T(8,128)(2,1)S(1)} %broadcast_in_dim.138, bf16[4,2432,128]{1,2,0:T(8,128)(2,1)S(1)} %fusion.49, bf16[4,384,32]{1,2,0:T(8,128)(2,1)S(1)} %get-tuple-element.22, bf16[4,384,32]{1,2,0:T(8,128)(2,1)S(1)} %get-tuple-element.21, bf16[4,384,128]{1,2,0:T(8,128)(2,1)S(1)} %slice.498), kind=kOutput, calls=%fused_computation.102 | convolution fusion | flops 1443692544 | bytes 19267584 | tf_op jit(solution)/shard_map/htd,hsd->hts/dot_general | solution.py:60
  419.3 20.3 %fusion.181 = (f32[4,384]{1,0:T(4,128)S(1)}, f32[4,384,2432]{2,1,0:T(8,128)}) fusion(f32[4,384,2432]{2,1,0:T(8,128)} %fusion.70, pred[384,2432]{1,0:T(8,128)(4,1)S(1)} %iota_compare_fusion), kind=kOutput, calls=%fused_computation.285 | output fusion | flops 22415744 | bytes 30824448 | tf_op jit(solution)/shard_map/sub | solution.py:63
  439.7 9.9 %fusion.77 = bf16[4,128,384]{2,1,0:T(8,128)(2,1)S(1)} fusion(f32[4,384,2432]{2,1,0:T(8,128)} %get-tuple-element.66, f32[4,384]{1,0:T(4,128)S(1)} %get-tuple-element.65, bf16[6,2432,512]{2,1,0:T(8,128)(2,1)} %dynamic_update_slice.41, bf16[512,4,128]{2,1,0:T(4,128)(2,1)} %param.28), kind=kOutput, calls=%fused_computation.121 | convolution fusion | flops 2240282624 | bytes 18356224 | tf_op jit(solution)/shard_map/hts,hsv->thv/dot_general | solution.py:64
  449.5 9.1 %fusion.187 = f32[384,6144]{1,0:T(8,128)} fusion(bf16[384,512]{0,1:T(8,128)(2,1)S(1)} %bitcast.273, bf16[512,6144]{1,0:T(8,128)(2,1)} %param.29), kind=kOutput, calls=%fused_computation.291 | convolution fusion | flops 2415919104 | bytes 16121856 | tf_op jit(solution)/shard_map/dot_general | solution.py:20
  466.3 60.6 %reduce-scatter.15.cloned.1.call-done = f32[24,6144]{1,0:T(8,128)} async-done(((f32[384,6144]{1,0:T(8,128)}), f32[24,6144]{1,0:T(8,128)}) %reduce-scatter.15.cloned.1.call-update) | async-done | bytes 589840 | tf_op jit(solution)/shard_map/reduce_scatter | solution.py:66
  528.8 69.0 %reduce-scatter.17.cloned.1.call-done = f32[24,6144]{1,0:T(8,128)} async-done(((f32[384,6144]{1,0:T(8,128)}), f32[24,6144]{1,0:T(8,128)}) %reduce-scatter.17.cloned.1.call-update) | async-done | bytes 589840 | tf_op jit(solution)/shard_map/reduce_scatter | solution.py:66
  (166 shorter events, 112.8 us)
Async XLA Ops:
  7.2 116.3 %copy-start = (bf16[1536,4,192]{0,2,1:T(8,128)(2,1)S(1)}, bf16[1536,4,192]{0,2,1:T(8,128)(2,1)}, u32[]{:S(2)}) copy-start(bf16[1536,4,192]{0,2,1:T(8,128)(2,1)} %param.26) | copy-start | bytes 7077892
  7.2 68.7 %all-gather.3.cloned.1.call-start = ((), (), s32[]{:S(2)}) async-start(), calls=%async_computation.6 | async-start | bytes 3133440 | tf_op jit(solution)/shard_map/all_gather | solution.py:42
  7.3 13.8 %copy-start.4 = (bf16[6,2432,64]{1,2,0:T(8,128)(2,1)S(1)}, bf16[6,2432,64]{1,2,0:T(8,128)(2,1)}, u32[]{:S(2)}) copy-start(bf16[6,2432,64]{1,2,0:T(8,128)(2,1)} %param.20) | copy-start | bytes 5603332
  21.1 3.6 copy-start.26
  26.7 6.3 %copy-start.1 = (bf16[6,24,6144]{2,1,0:T(8,128)(2,1)}, bf16[6,24,6144]{2,1,0:T(8,128)(2,1)S(1)}, u32[]{:S(2)}) copy-start(bf16[6,24,6144]{2,1,0:T(8,128)(2,1)S(1)} %fusion.76) | copy-start | bytes 5308420
  26.7 6.5 %copy-start.29 = (f32[512]{0:T(512)S(1)}, f32[512]{0:T(512)}, u32[]{:S(2)}) copy-start(f32[512]{0:T(512)} %param.25) | copy-start | bytes 6148
  34.1 89.3 %all-gather.5.cloned.1.call-start = ((), (), s32[]{:S(2)}) async-start(), calls=%async_computation.7 | async-start | bytes 7520256 | tf_op jit(solution)/shard_map/all_gather | solution.py:43
  34.2 8.7 %copy-start.28 = (f32[1536]{0:T(1024)S(1)}, f32[1536]{0:T(1024)}, u32[]{:S(2)}) copy-start(f32[1536]{0:T(1024)} %param.23) | copy-start | bytes 18436
  34.2 9.8 %copy-start.27 = (s32[6]{0:T(128)S(1)}, s32[6]{0:T(128)}, u32[]{:S(2)}) copy-start(s32[6]{0:T(128)} %param.16) | copy-start | bytes 76
  43.9 414.8 %reduce-scatter.7.cloned.1.call-start = ((), (), s32[]{:S(2)}) async-start(), calls=%async_computation.8 | async-start | bytes 10027008 | tf_op jit(solution)/shard_map/reduce_scatter | solution.py:66
  114.8 5.0 copy-start.2
  126.1 2.9 copy-start.22
  126.1 2.9 copy-start.23
  126.1 2.9 copy-start.24
  126.1 2.9 copy-start.25
  126.2 3.0 copy-start.7
  126.2 3.8 copy-start.3
  178.6 282.0 %reduce-scatter.9.cloned.1.call-start = ((), (), s32[]{:S(2)}) async-start(), calls=%async_computation.9 | async-start | bytes 10027008 | tf_op jit(solution)/shard_map/reduce_scatter | solution.py:66
  233.1 229.4 %reduce-scatter.11.cloned.1.call-start = ((), (), s32[]{:S(2)}) async-start(), calls=%async_computation.10 | async-start | bytes 10027008 | tf_op jit(solution)/shard_map/reduce_scatter | solution.py:66
  241.6 2.8 copy-start.18
  241.6 2.8 copy-start.19
  241.6 2.8 copy-start.20
  293.1 171.3 %reduce-scatter.13.cloned.1.call-start = ((), (), s32[]{:S(2)}) async-start(), calls=%async_computation.11 | async-start | bytes 10027008 | tf_op jit(solution)/shard_map/reduce_scatter | solution.py:66
  300.1 7.6 %copy-start.8 = (pred[384,2432]{1,0:T(8,128)(4,1)S(1)}, pred[384,2432]{1,0:T(8,128)(4,1)}, u32[]{:S(2)}) copy-start(pred[384,2432]{1,0:T(8,128)(4,1)} %iota_compare_fusion.2) | copy-start | bytes 2801668
  346.9 180.0 %reduce-scatter.15.cloned.1.call-start = ((), (), s32[]{:S(2)}) async-start(), calls=%async_computation.12 | async-start | bytes 10027008 | tf_op jit(solution)/shard_map/reduce_scatter | solution.py:66
  354.5 2.8 copy-start.14
  354.5 2.8 copy-start.15
  354.5 2.8 copy-start.16
  354.5 2.8 copy-start.17
  354.6 2.9 copy-start.6
  405.6 192.2 %reduce-scatter.17.cloned.1.call-start = ((), (), s32[]{:S(2)}) async-start(), calls=%async_computation.13 | async-start | bytes 10027008 | tf_op jit(solution)/shard_map/reduce_scatter | solution.py:66
  407.0 4.6 copy-start.5
  (8 other events, 13.5 us)
Sparse Core Ops, SparseCore 0:
  34.2 41.6 all-gather.2
  78.2 45.2 all-gather.4
  178.7 64.9 reduce-scatter.6
  245.9 68.5 reduce-scatter.8
  316.7 68.4 reduce-scatter.10
  387.4 68.5 reduce-scatter.12
  458.3 68.4 reduce-scatter.14
  529.2 68.4 reduce-scatter.16
